TPU v7x, 32 devices: a whole 2x2x4 slice. The times are simulated.
32 devices in a mesh: tm: 8 (over z, core), member: 4 (over y, x).
Axes of the slice: x: 2, y: 2, z: 4, core: 2. Of those that a mesh axis runs over, the one named last changes fastest.
Arguments:
- fields: float32 [48, 48, 8192], P('member', 'tm'), may hold values from 200 to 350, as said below
Outputs:
- covariance: float32 [48, 48, 8192], P('member', None, 'tm')
Inputs may be any that keep to these rules, and one draw needn't show every extreme that they name: `fields`: month t is calendar month t mod 12.
All inputs are finite; a program needn't handle non-finite values.
Results may differ from a plain program's by a relative error of at most 0.0003.
Values sent between devices are 32-bit elements; how exact they have to be, the bound alone decides.
No kernel may reach another device: no remote copies, remote signals or barrier semaphores. Data moves between devices by JAX's collectives and lax.ppermute only.
A program may use at most 192 MiB of HBM per device.

v0:
```python
import functools
import math

import jax
import jax.numpy as jnp
from jax import lax
from jax.experimental import pallas as pl
from jax.experimental.pallas import tpu as pltpu
from jax.sharding import PartitionSpec as P


LANES = 128
FOLD = 2
PART = LANES // FOLD
YEAR = 12
VMEM_LIMIT = 48 * 1024 * 1024


def low_lanes(rows):
    return lax.broadcasted_iota(jnp.int32, (rows, LANES), 1) < PART


def split_lanes(a, b, low):
    return jnp.where(low, a, pltpu.roll(b, PART, 1)), jnp.where(low, pltpu.roll(a, PART, 1), b)


def pack_kernel(tm, halves, groups, block, width, chunks, x_ref, *refs):
    first_refs, kept_ref, other_ref, held = refs[:tm], refs[tm], refs[tm + 1], refs[tm + 2]
    me = lax.axis_index("tm")
    at_group = lax.axis_index("member")
    members, months = x_ref.shape[0], x_ref.shape[1]
    steps = months // FOLD
    rows = members * steps
    low = low_lanes(rows)

    def rows_of(k, lane, times):
        lanes = pl.ds(pl.multiple_of((me ^ k) * block + lane, LANES), LANES)
        return jnp.concatenate([x_ref[:, t, lanes] for t in times], axis=0)

    for k in range(tm):
        for lane in range(0, width, LANES):
            first_refs[k][:, lane : lane + LANES] = rows_of(k, lane, range(months))
    size = (tm // halves) * rows
    for c in range(1, chunks):
        for h, out_ref in enumerate((kept_ref, other_ref)):
            for y in range(tm // halves):
                at_rows = slice(y * rows, (y + 1) * rows)
                for p in range(groups // FOLD):
                    lane = c * width + p * LANES
                    a = rows_of(y * halves + h, lane, range(steps))
                    b = rows_of(y * halves + h, lane, range(steps, months))
                    held[FOLD * p, at_rows, :], held[FOLD * p + 1, at_rows, :] = split_lanes(a, b, low)
            for d in range(groups):
                row = ((c - 1) * groups + d) * size
                out_ref[row : row + size, :] = held[at_group ^ d]


def merge_kernel(groups, sets, kept_ref, other_ref, *out_refs):
    size = kept_ref.shape[0] // (groups * sum(len(s) for s in sets))
    for n, chunk_set in enumerate(sets):
        for d in range(groups):
            for i, c in enumerate(chunk_set):
                row = ((c - 1) * groups + d) * size
                for h, in_ref in enumerate((kept_ref, other_ref)):
                    to = (i * 2 + h) * size
                    out_refs[n * groups + d][to : to + size, :] = in_ref[row : row + size, :]


def repack_kernel(years, halves, groups, members, count, *refs):
    in_refs, out_refs, held = refs[:groups], refs[groups:-1], refs[-1]
    me = lax.axis_index("member")
    whole = groups * members
    rows = in_refs[0].shape[0] // (count * halves * years)
    steps = rows // members
    for d in range(groups):
        held[me ^ d] = in_refs[d][...]
    for c in range(count):
        for y in range(years):
            for h in range(halves):
                for t in range(steps):
                    row = ((c * halves + h) * years + y) * rows + t * members
                    to = (h * steps + t) * whole
                    out_refs[c * years + y][to : to + whole, :] = jnp.concatenate(
                        [held[m, row : row + members, :] for m in range(groups)], axis=0
                    )


def contrasts(by_year, norm):
    out = []
    for k in range(1, len(by_year)):
        total = by_year[k] - by_year[0]
        for j in range(1, k):
            total = total + (by_year[k] - by_year[j])
        out.append(total * (1.0 / math.sqrt(k * (k + 1) * norm)))
    return out


def contrast_kernel(halves, groups, norm, *refs):
    tm = len(refs) - groups - 2
    in_refs, out_refs, held = refs[:tm], refs[tm + 1 : tm + 1 + groups], refs[-1]
    me = lax.axis_index("member")
    rows = in_refs[0].shape[0]
    low = low_lanes(rows)
    for p in range(groups // FOLD):
        lanes = slice(p * LANES, (p + 1) * LANES)
        first, second = (
            contrasts([in_refs[k][:, lanes] for k in range(h, tm, halves)], norm) for h in range(halves)
        )
        for k, (a, b) in enumerate(zip(first, second)):
            at_rows = slice(k * rows, (k + 1) * rows)
            held[FOLD * p, at_rows, :], held[FOLD * p + 1, at_rows, :] = split_lanes(a, b, low)
    for d in range(groups):
        out_refs[d][...] = held[me ^ d]


def transposed(block):
    sublane = lax.broadcasted_iota(jnp.int32, (8, LANES), 0)
    for step in (4, 2, 1):
        keep = (sublane & step) == 0
        new = list(block)
        for s in range(8):
            if not s & step:
                a, b = block[s], block[s + step]
                new[s] = jnp.where(keep, a, pltpu.roll(b, step, 0))
                new[s + step] = jnp.where(keep, pltpu.roll(a, 8 - step, 0), b)
        block = new
    return block


def products(members, joined, full, out_refs):
    me = lax.axis_index("member")
    steps, whole = joined.shape[0], joined.shape[1]
    tiles = whole // 8
    low = low_lanes(8)
    planes = members // FOLD

    def at(row, tile):
        first = (row % members) * whole + 8 * tile
        return row // members, slice(first, first + 8), slice(None)

    for i in range(tiles):
        most = max(1, min(8, 24 // (tiles - i)))
        for first in range(0, 8, most):
            rows = range(8 * i + first, 8 * i + min(8, first + most))
            sums = {}
            for t in range(steps):
                right = {j: joined[t, 8 * j : 8 * j + 8, :] for j in range(i, tiles)}
                for r in rows:
                    left = jnp.broadcast_to(joined[t, r : r + 1, :], (8, LANES))
                    for j in range(i, tiles):
                        term = left * right[j]
                        sums[r, j] = term if t == 0 else sums[r, j] + term
            for (r, j), x in sums.items():
                full[at(r, j)] = x + pltpu.roll(x, PART, 1)
    for i in range(tiles):
        for j in range(i + 1, tiles):
            block = [full[at(8 * i + s, j)] for s in range(8)]
            for s, value in enumerate(transposed(block)):
                full[at(8 * j + s, i)] = value
    for d in range(len(out_refs)):
        m = me ^ d
        for a in range(planes):
            for j in range(tiles):
                x, y = (full[m, u * whole + 8 * j : u * whole + 8 * j + 8, :] for u in (a, a + planes))
                out_refs[d][a, 8 * j : 8 * j + 8, :] = jnp.where(low, x, y)


def group_products_kernel(groups, members, *refs):
    in_refs, out_refs = refs[:groups], refs[groups : 2 * groups]
    held, joined, full = refs[2 * groups :]
    me = lax.axis_index("member")
    for d in range(groups):
        held[me ^ d] = in_refs[d][...]
    for t in range(joined.shape[0]):
        joined[t] = jnp.concatenate(
            [held[m, t * members : (t + 1) * members, :] for m in range(groups)], axis=0
        )
    products(members, joined, full, out_refs)


def fill(joined, in_refs, whole, norm):
    per_year = in_refs[0].shape[0] // whole
    for t in range(per_year):
        values = [in_ref[t * whole : (t + 1) * whole, :] for in_ref in in_refs]
        for k, value in enumerate(contrasts(values, norm)):
            joined[k * per_year + t] = value


def block_products_kernel(years, groups, members, norm, *refs):
    in_refs, out_refs = refs[:years], refs[years : years + groups]
    joined, full = refs[years + groups :]
    fill(joined, in_refs, groups * members, norm)
    products(members, joined, full, out_refs)


def farthest_products_kernel(years, groups, members, norm, *refs):
    in_refs, joined, out_ref = refs[:years], refs[years], refs[years + 1]
    fill(joined, in_refs, groups * members, norm)
    first = (lax.axis_index("member") ^ (groups - 1)) * members
    planes, tiles = members // FOLD, groups * members // 8
    low = low_lanes(8)
    for a in range(0, planes, 2):
        rows = [u + s * planes for u in range(a, min(a + 2, planes)) for s in range(FOLD)]
        sums = {}
        for t in range(joined.shape[0]):
            right = [joined[t, 8 * j : 8 * j + 8, :] for j in range(tiles)]
            for r in rows:
                left = jnp.broadcast_to(joined[t, pl.ds(first + r, 1), :], (8, LANES))
                for j in range(tiles):
                    term = left * right[j]
                    sums[r, j] = term if t == 0 else sums[r, j] + term
        for u in range(a, min(a + 2, planes)):
            for j in range(tiles):
                x, y = sums[u, j], sums[u + planes, j]
                out_ref[u, 8 * j : 8 * j + 8, :] = jnp.where(
                    low, x + pltpu.roll(x, PART, 1), y + pltpu.roll(y, PART, 1)
                )


def other_products_kernel(members, *refs):
    products(members, refs[0], refs[-1], refs[1:-1])


def place_kernel(groups, *refs):
    in_refs, out_ref, held = refs[:groups], refs[-2], refs[-1]
    me = lax.axis_index("member")
    for d in range(groups):
        held[me ^ d] = in_refs[d][...]
    planes, whole = in_refs[0].shape[0], in_refs[0].shape[1]
    low = low_lanes(whole)
    for p in range(groups // FOLD):
        lanes = slice(p * LANES, (p + 1) * LANES)
        for i in range(planes):
            out_ref[i, :, lanes], out_ref[i + planes, :, lanes] = split_lanes(
                held[FOLD * p, i], held[FOLD * p + 1, i], low
            )


def call(kernel, outs, flops, *args, scratch=()):
    nbytes = 4 * (sum(math.prod(o) for o in outs) + sum(a.size for a in args))
    return pl.pallas_call(
        kernel,
        out_shape=[jax.ShapeDtypeStruct(o, jnp.float32) for o in outs],
        in_specs=[pl.BlockSpec(memory_space=pltpu.VMEM)] * len(args),
        out_specs=[pl.BlockSpec(memory_space=pltpu.VMEM)] * len(outs),
        scratch_shapes=[pltpu.VMEM(s, jnp.float32) for s in scratch],
        compiler_params=pltpu.CompilerParams(vmem_limit_bytes=VMEM_LIMIT),
        cost_estimate=pl.CostEstimate(flops=int(flops), bytes_accessed=nbytes, transcendentals=0),
    )(*args)


def gate_kernel(x_ref, out_ref):
    out_ref[...] = x_ref[:8, :LANES]


def swap(x, axis, k):
    return lax.ppermute(x, axis, [(i, i ^ k) for i in range(lax.axis_size(axis))])


def swap_all(pieces, axis, stride):
    out = dict(enumerate(pieces[:1]))
    for k in reversed(range(1, len(pieces))):
        out[k] = swap(pieces[k], axis, k * stride)
    return [out[k] for k in range(len(pieces))]


def chunk_sets(chunks):
    sets = [[1], list(range(2, chunks))]
    return [s for s in sets if s]


def per_device(fields):
    members, months, pixels = fields.shape
    tm, groups = lax.axis_size("tm"), lax.axis_size("member")
    halves = YEAR // months
    years = tm // halves
    block = pixels // tm
    width = PART * groups
    chunks = block // width
    whole = members * groups
    rows = members * months
    part_rows = rows // FOLD
    norm = float(months * tm - YEAR)
    sets = chunk_sets(chunks)
    assert halves == 2 and months % FOLD == 0 and members % FOLD == 0 and block == chunks * width

    both = ((chunks - 1) * groups * years * part_rows, LANES)
    packed = call(
        functools.partial(pack_kernel, tm, halves, groups, block, width, chunks),
        [(rows, width)] * tm + [both] * 2, 4e6, fields,
        scratch=[(groups, years * part_rows, LANES)],
    )
    by_block, kept, other = packed[:tm], packed[tm], packed[tm + 1]
    other = swap(other, "tm", 1)
    arrived = {0: by_block[0]}
    for k in sorted(range(1, tm), key=lambda k: (-(k // halves), k)):
        far = k >= tm - halves
        arrived[k] = swap(by_block[k], "tm", k)
    arrived = [arrived[k] for k in range(tm)]

    merged = call(
        functools.partial(merge_kernel, groups, sets),
        [(len(s) * halves * years * part_rows, LANES) for s in sets for _ in range(groups)],
        1e6, kept, other,
    )
    by_year = {}
    for n, chunk_set in enumerate(sets):
        near = swap_all(merged[n * groups : (n + 1) * groups], "member", 1)
        mine = call(
            functools.partial(repack_kernel, years, halves, groups, members, len(chunk_set)),
            [(halves * part_rows * groups, LANES)] * (years * len(chunk_set)),
            1e6, *near, scratch=[(groups, *near[0].shape)],
        )
        for i, c in enumerate(chunk_set):
            by_year[c] = swap_all(mine[i * years : (i + 1) * years], "tm", halves)

    gate = call(gate_kernel, [(8, LANES)], 1e5, by_block[0])[0]
    total = (years - 1) * halves * part_rows
    result = [(members // FOLD, whole, LANES)] * groups
    tail = [(total // members, whole, LANES), (groups, members * whole, LANES)]
    parts = []
    for c in range(chunks):
        if c == 0:
            sent = call(
                functools.partial(contrast_kernel, halves, groups, norm),
                [(total, LANES)] * groups, 4e6, *arrived, gate,
                scratch=[(groups, total, LANES)],
            )
            here = swap_all(sent, "member", 1)
            summed = call(
                functools.partial(group_products_kernel, groups, members),
                result, 1e7, *here, scratch=[(groups, total, LANES)] + tail,
            )
        elif c == chunks - 1:
            joined, far = call(
                functools.partial(farthest_products_kernel, years, groups, members, norm),
                [tail[0], result[0]], 3e6, *by_year[c],
            )
            far = swap(far, "member", groups - 1)
            summed = call(
                functools.partial(other_products_kernel, members),
                result[1:], 1e7, joined, scratch=tail[1:],
            )
            parts.append(swap_all(summed, "member", 1) + [far])
            continue
        else:
            summed = call(
                functools.partial(block_products_kernel, years, groups, members, norm),
                result, 1e7, *by_year[c], scratch=tail,
            )
        parts.append(swap_all(summed, "member", 1))

    out = []
    for c in range(chunks):
        out = [
            pl.pallas_call(
                functools.partial(place_kernel, groups),
                out_shape=jax.ShapeDtypeStruct((members, whole, block), jnp.float32),
                grid=(1,),
                in_specs=[pl.BlockSpec(memory_space=pltpu.VMEM)] * groups
                + [pl.BlockSpec(memory_space=pl.ANY)] * len(out),
                out_specs=pl.BlockSpec((members, whole, width), lambda i, c=c: (0, 0, c)),
                scratch_shapes=[pltpu.VMEM((groups, members // FOLD, whole, LANES), jnp.float32)],
                input_output_aliases={groups: 0} if out else {},
                compiler_params=pltpu.CompilerParams(vmem_limit_bytes=VMEM_LIMIT),
                cost_estimate=pl.CostEstimate(
                    flops=1000000, bytes_accessed=8 * members * whole * width, transcendentals=0
                ),
            )(*parts[c], *out)
        ]
    return out[0]


def solution(mesh):
    in_specs = (P("member", "tm", None),)
    out_specs = P("member", None, "tm")

    return jax.shard_map(per_device, mesh=mesh, in_specs=in_specs, out_specs=out_specs, check_vma=False)
```

profile of v0, /device:TPU:8, one launch (start us, length us, event | category | flops | bytes accessed | tf_op | source)
XLA Modules:
  0.0 109.7 jit_solution(13392597030836841806)
XLA Ops:
  0.0 1.9 %copy-done = f32[12,6,8192]{2,1,0:T(8,128)S(1)} copy-done((f32[12,6,8192]{2,1,0:T(8,128)S(1)}, f32[12,6,8192]{2,1,0:T(8,128)}, u32[]{:S(2)}) %copy-start) | copy-done | bytes 2359320
  3.7 1.4 %collective-permute-start.27 = (f32[72,256]{1,0:T(8,128)S(1)}, f32[72,256]{1,0:T(8,128)S(1)}, u32[]{:S(2)}, u32[]{:S(2)}) collective-permute-start(f32[72,256]{1,0:T(8,128)S(1)} %get-tuple-element.94), channel_id=1, source_target_pairs={{0,12},{4,8},{8,4},{12,0},{16,28},{20,24},{24,20},{28,16},{1,13},{... | collective-permute-start | bytes 221192 | tf_op jit(solution)/shard_map/ppermute | solution.py:257
  5.7 1.6 %collective-permute-start.16 = (f32[288,128]{1,0:T(8,128)S(1)}, f32[288,128]{1,0:T(8,128)S(1)}, u32[]{:S(2)}, u32[]{:S(2)}) collective-permute-start(f32[288,128]{1,0:T(8,128)S(1)} %get-tuple-element.80), channel_id=1, source_target_pairs={{0,1},{1,0},{2,3},{3,2},{4,5},{5,4},{6,7},{7,6},{8,9},{9,8},{10,11... | collective-permute-start | bytes 442376 | tf_op jit(solution)/shard_map/ppermute | solution.py:257
  7.3 2.6 %collective-permute-start.28 = (f32[72,256]{1,0:T(8,128)S(1)}, f32[72,256]{1,0:T(8,128)S(1)}, u32[]{:S(2)}, u32[]{:S(2)}) collective-permute-start(f32[72,256]{1,0:T(8,128)S(1)} %get-tuple-element.95), channel_id=1, source_target_pairs={{0,16},{4,20},{8,24},{12,28},{16,0},{20,4},{24,8},{28,12},{1,17},{... | collective-permute-start | bytes 221192 | tf_op jit(solution)/shard_map/ppermute | solution.py:257
  10.5 1.5 %collective-permute-start.2 = (f32[576,128]{1,0:T(8,128)S(1)}, f32[576,128]{1,0:T(8,128)S(1)}, u32[]{:S(2)}, u32[]{:S(2)}) collective-permute-start(f32[576,128]{1,0:T(8,128)S(1)} %get-tuple-element.60), channel_id=1, source_target_pairs={{0,2},{1,3},{2,0},{3,1},{4,6},{5,7},{6,4},{7,5},{8,10},{9,11},{10,... | collective-permute-start | bytes 884744 | tf_op jit(solution)/shard_map/ppermute | solution.py:257
  12.0 2.6 %collective-permute-done.28.refs_4_ = f32[72,256]{1,0:T(8,128)S(1)} collective-permute-done((f32[72,256]{1,0:T(8,128)S(1)}, f32[72,256]{1,0:T(8,128)S(1)}, u32[]{:S(2)}, u32[]{:S(2)}) %collective-permute-start.28) | collective-permute-done | bytes 73760 | tf_op jit(solution)/shard_map/ppermute | solution.py:257
  14.6 1.5 %collective-permute-start.17 = (f32[288,128]{1,0:T(8,128)S(1)}, f32[288,128]{1,0:T(8,128)S(1)}, u32[]{:S(2)}, u32[]{:S(2)}) collective-permute-start(f32[288,128]{1,0:T(8,128)S(1)} %get-tuple-element.81), channel_id=1, source_target_pairs={{0,2},{1,3},{2,0},{3,1},{4,6},{5,7},{6,4},{7,5},{8,10},{9,11},{10,... | collective-permute-start | bytes 442376 | tf_op jit(solution)/shard_map/ppermute | solution.py:257
  16.2 1.5 %collective-permute-start.18 = (f32[288,128]{1,0:T(8,128)S(1)}, f32[288,128]{1,0:T(8,128)S(1)}, u32[]{:S(2)}, u32[]{:S(2)}) collective-permute-start(f32[288,128]{1,0:T(8,128)S(1)} %get-tuple-element.82), channel_id=1, source_target_pairs={{0,3},{1,2},{2,1},{3,0},{4,7},{5,6},{6,5},{7,4},{8,11},{9,10},{10,... | collective-permute-start | bytes 442376 | tf_op jit(solution)/shard_map/ppermute | solution.py:257
  17.6 1.5 %collective-permute-start.3 = (f32[576,128]{1,0:T(8,128)S(1)}, f32[576,128]{1,0:T(8,128)S(1)}, u32[]{:S(2)}, u32[]{:S(2)}) collective-permute-start(f32[576,128]{1,0:T(8,128)S(1)} %get-tuple-element.61), channel_id=1, source_target_pairs={{0,3},{1,2},{2,1},{3,0},{4,7},{5,6},{6,5},{7,4},{8,11},{9,10},{10,... | collective-permute-start | bytes 884744 | tf_op jit(solution)/shard_map/ppermute | solution.py:257
  19.1 13.0 %collective-permute-done.17.refs_2_ = f32[288,128]{1,0:T(8,128)S(1)} collective-permute-done((f32[288,128]{1,0:T(8,128)S(1)}, f32[288,128]{1,0:T(8,128)S(1)}, u32[]{:S(2)}, u32[]{:S(2)}) %collective-permute-start.17) | collective-permute-done | bytes 147488 | tf_op jit(solution)/shard_map/ppermute | solution.py:257
  32.1 1.6 %collective-permute-start.30 = (f32[72,256]{1,0:T(8,128)S(1)}, f32[72,256]{1,0:T(8,128)S(1)}, u32[]{:S(2)}, u32[]{:S(2)}) collective-permute-start(f32[72,256]{1,0:T(8,128)S(1)} %get-tuple-element.97), channel_id=1, source_target_pairs={{0,24},{4,28},{8,16},{12,20},{16,8},{20,12},{24,0},{28,4},{1,25},{... | collective-permute-start | bytes 221192 | tf_op jit(solution)/shard_map/ppermute | solution.py:257
  33.8 5.0 %collective-permute-done.30.refs_6_ = f32[72,256]{1,0:T(8,128)S(1)} collective-permute-done((f32[72,256]{1,0:T(8,128)S(1)}, f32[72,256]{1,0:T(8,128)S(1)}, u32[]{:S(2)}, u32[]{:S(2)}) %collective-permute-start.30) | collective-permute-done | bytes 73760 | tf_op jit(solution)/shard_map/ppermute | solution.py:257
  40.5 1.6 %collective-permute-start.32 = (f32[216,128]{1,0:T(8,128)S(1)}, f32[216,128]{1,0:T(8,128)S(1)}, u32[]{:S(2)}, u32[]{:S(2)}) collective-permute-start(f32[216,128]{1,0:T(8,128)S(1)} %get-tuple-element.100), channel_id=1, source_target_pairs={{0,1},{1,0},{2,3},{3,2},{4,5},{5,4},{6,7},{7,6},{8,9},{9,8},{10,11... | collective-permute-start | bytes 331784 | tf_op jit(solution)/shard_map/ppermute | solution.py:257
  42.0 1.5 %collective-permute-start.33 = (f32[216,128]{1,0:T(8,128)S(1)}, f32[216,128]{1,0:T(8,128)S(1)}, u32[]{:S(2)}, u32[]{:S(2)}) collective-permute-start(f32[216,128]{1,0:T(8,128)S(1)} %get-tuple-element.101), channel_id=1, source_target_pairs={{0,2},{1,3},{2,0},{3,1},{4,6},{5,7},{6,4},{7,5},{8,10},{9,11},{10,... | collective-permute-start | bytes 331784 | tf_op jit(solution)/shard_map/ppermute | solution.py:257
  44.0 2.7 %collective-permute-start.20 = (f32[288,128]{1,0:T(8,128)S(1)}, f32[288,128]{1,0:T(8,128)S(1)}, u32[]{:S(2)}, u32[]{:S(2)}) collective-permute-start(f32[288,128]{1,0:T(8,128)S(1)} %get-tuple-element.85), channel_id=1, source_target_pairs={{0,16},{4,20},{8,24},{12,28},{16,0},{20,4},{24,8},{28,12},{1,17},{... | collective-permute-start | bytes 442376 | tf_op jit(solution)/shard_map/ppermute | solution.py:257
  47.8 1.7 %collective-permute-done.33.refs_2_ = f32[216,128]{1,0:T(8,128)S(1)} collective-permute-done((f32[216,128]{1,0:T(8,128)S(1)}, f32[216,128]{1,0:T(8,128)S(1)}, u32[]{:S(2)}, u32[]{:S(2)}) %collective-permute-start.33) | collective-permute-done | bytes 110624 | tf_op jit(solution)/shard_map/ppermute | solution.py:257
  50.0 2.8 %collective-permute-start.11 = (f32[288,128]{1,0:T(8,128)S(1)}, f32[288,128]{1,0:T(8,128)S(1)}, u32[]{:S(2)}, u32[]{:S(2)}) collective-permute-start(f32[288,128]{1,0:T(8,128)S(1)} %get-tuple-element.73), channel_id=1, source_target_pairs={{0,16},{4,20},{8,24},{12,28},{16,0},{20,4},{24,8},{28,12},{1,17},{... | collective-permute-start | bytes 442376 | tf_op jit(solution)/shard_map/ppermute | solution.py:257
  53.0 1.4 %shard_map.27 = (f32[6,48,128]{2,1,0:T(8,128)S(1)}, f32[6,48,128]{2,1,0:T(8,128)S(1)}, f32[6,48,128]{2,1,0:T(8,128)S(1)}, f32[6,48,128]{2,1,0:T(8,128)S(1)}) custom-call(f32[216,128]{1,0:T(8,128)S(1)} %get-tuple-element.99.refs_0_, f32[216,128]{1,0:T(8,128)S(1)} %collective-permute-done.32.refs_1_, f32[216,128]{1,0:T(8,128)S(1)} %collective-permute-done.33.refs_2_, ...), custom_call_target="tpu_custom_call" | custom-call | flops 10000000 | bytes 1032192 | tf_op jit(solution)/shard_map/pallas_call | solution.py:241
  54.4 2.3 %collective-permute-done.20.refs_2_ = f32[288,128]{1,0:T(8,128)S(1)} collective-permute-done((f32[288,128]{1,0:T(8,128)S(1)}, f32[288,128]{1,0:T(8,128)S(1)}, u32[]{:S(2)}, u32[]{:S(2)}) %collective-permute-start.20) | collective-permute-done | bytes 147488 | tf_op jit(solution)/shard_map/ppermute | solution.py:257
  56.7 1.9 %collective-permute-start.35 = (f32[6,48,128]{2,1,0:T(8,128)S(1)}, f32[6,48,128]{2,1,0:T(8,128)S(1)}, u32[]{:S(2)}, u32[]{:S(2)}) collective-permute-start(f32[6,48,128]{2,1,0:T(8,128)S(1)} %get-tuple-element.104), channel_id=1, source_target_pairs={{0,1},{1,0},{2,3},{3,2},{4,5},{5,4},{6,7},{7,6},{8,9},{9,8},{10,11... | collective-permute-start | bytes 442376 | tf_op jit(solution)/shard_map/ppermute | solution.py:257
  58.6 7.4 %collective-permute-done.21.refs_3_ = f32[288,128]{1,0:T(8,128)S(1)} collective-permute-done((f32[288,128]{1,0:T(8,128)S(1)}, f32[288,128]{1,0:T(8,128)S(1)}, u32[]{:S(2)}, u32[]{:S(2)}) %collective-permute-start.21) | collective-permute-done | bytes 147488 | tf_op jit(solution)/shard_map/ppermute | solution.py:257
  66.1 1.5 %collective-permute-start.36 = (f32[6,48,128]{2,1,0:T(8,128)S(1)}, f32[6,48,128]{2,1,0:T(8,128)S(1)}, u32[]{:S(2)}, u32[]{:S(2)}) collective-permute-start(f32[6,48,128]{2,1,0:T(8,128)S(1)} %get-tuple-element.105), channel_id=1, source_target_pairs={{0,2},{1,3},{2,0},{3,1},{4,6},{5,7},{6,4},{7,5},{8,10},{9,11},{10,... | collective-permute-start | bytes 442376 | tf_op jit(solution)/shard_map/ppermute | solution.py:257
  68.7 3.4 %collective-permute-start.5 = (f32[288,128]{1,0:T(8,128)S(1)}, f32[288,128]{1,0:T(8,128)S(1)}, u32[]{:S(2)}, u32[]{:S(2)}) collective-permute-start(f32[288,128]{1,0:T(8,128)S(1)} %get-tuple-element.64), channel_id=1, source_target_pairs={{0,16},{4,20},{8,24},{12,28},{16,0},{20,4},{24,8},{28,12},{1,17},{... | collective-permute-start | bytes 442376 | tf_op jit(solution)/shard_map/ppermute | solution.py:257
  73.2 7.5 %collective-permute-start.6 = (f32[288,128]{1,0:T(8,128)S(1)}, f32[288,128]{1,0:T(8,128)S(1)}, u32[]{:S(2)}, u32[]{:S(2)}) collective-permute-start(f32[288,128]{1,0:T(8,128)S(1)} %get-tuple-element.65), channel_id=1, source_target_pairs={{0,24},{4,28},{8,16},{12,20},{16,8},{20,12},{24,0},{28,4},{1,25},{... | collective-permute-start | bytes 442376 | tf_op jit(solution)/shard_map/ppermute | solution.py:257
  80.7 1.4 %shard_map.24 = (f32[6,48,128]{2,1,0:T(8,128)S(1)}, f32[6,48,128]{2,1,0:T(8,128)S(1)}, f32[6,48,128]{2,1,0:T(8,128)S(1)}, f32[6,48,128]{2,1,0:T(8,128)S(1)}) custom-call(f32[288,128]{1,0:T(8,128)S(1)} %get-tuple-element.83.refs_0_, f32[288,128]{1,0:T(8,128)S(1)} %collective-permute-done.19.refs_1_, f32[288,128]{1,0:T(8,128)S(1)} %collective-permute-done.20.refs_2_, ...), custom_call_target="tpu_custom_call" | custom-call | flops 10000000 | bytes 1179648 | tf_op jit(solution)/shard_map/pallas_call | solution.py:241
  82.1 1.4 %shard_map.22 = (f32[6,48,128]{2,1,0:T(8,128)S(1)}, f32[6,48,128]{2,1,0:T(8,128)S(1)}, f32[6,48,128]{2,1,0:T(8,128)S(1)}, f32[6,48,128]{2,1,0:T(8,128)S(1)}) custom-call(f32[288,128]{1,0:T(8,128)S(1)} %get-tuple-element.71.refs_0_, f32[288,128]{1,0:T(8,128)S(1)} %collective-permute-done.10.refs_1_, f32[288,128]{1,0:T(8,128)S(1)} %collective-permute-done.11.refs_2_, ...), custom_call_target="tpu_custom_call" | custom-call | flops 10000000 | bytes 1179648 | tf_op jit(solution)/shard_map/pallas_call | solution.py:241
  83.6 2.6 %collective-permute-start.37 = (f32[6,48,128]{2,1,0:T(8,128)S(1)}, f32[6,48,128]{2,1,0:T(8,128)S(1)}, u32[]{:S(2)}, u32[]{:S(2)}) collective-permute-start(f32[6,48,128]{2,1,0:T(8,128)S(1)} %get-tuple-element.106), channel_id=1, source_target_pairs={{0,3},{1,2},{2,1},{3,0},{4,7},{5,6},{6,5},{7,4},{8,11},{9,10},{10,... | collective-permute-start | bytes 442376 | tf_op jit(solution)/shard_map/ppermute | solution.py:257
  87.1 2.5 %collective-permute-start.24 = (f32[6,48,128]{2,1,0:T(8,128)S(1)}, f32[6,48,128]{2,1,0:T(8,128)S(1)}, u32[]{:S(2)}, u32[]{:S(2)}) collective-permute-start(f32[6,48,128]{2,1,0:T(8,128)S(1)} %get-tuple-element.90), channel_id=1, source_target_pairs={{0,3},{1,2},{2,1},{3,0},{4,7},{5,6},{6,5},{7,4},{8,11},{9,10},{10,... | collective-permute-start | bytes 442376 | tf_op jit(solution)/shard_map/ppermute | solution.py:257
  91.8 1.6 %collective-permute-start.7 = (f32[6,48,128]{2,1,0:T(8,128)S(1)}, f32[6,48,128]{2,1,0:T(8,128)S(1)}, u32[]{:S(2)}, u32[]{:S(2)}) collective-permute-start(f32[6,48,128]{2,1,0:T(8,128)S(1)} %get-tuple-element.68), channel_id=1, source_target_pairs={{0,1},{1,0},{2,3},{3,2},{4,5},{5,4},{6,7},{7,6},{8,9},{9,8},{10,11... | collective-permute-start | bytes 442376 | tf_op jit(solution)/shard_map/ppermute | solution.py:257
  95.0 2.9 %collective-permute-start.15 = (f32[6,48,128]{2,1,0:T(8,128)S(1)}, f32[6,48,128]{2,1,0:T(8,128)S(1)}, u32[]{:S(2)}, u32[]{:S(2)}) collective-permute-start(f32[6,48,128]{2,1,0:T(8,128)S(1)} %get-tuple-element.78), channel_id=1, source_target_pairs={{0,3},{1,2},{2,1},{3,0},{4,7},{5,6},{6,5},{7,4},{8,11},{9,10},{10,... | collective-permute-start | bytes 442376 | tf_op jit(solution)/shard_map/ppermute | solution.py:257
  99.1 1.7 %collective-permute-done.13.refs_1_ = f32[6,48,128]{2,1,0:T(8,128)S(1)} collective-permute-done((f32[6,48,128]{2,1,0:T(8,128)S(1)}, f32[6,48,128]{2,1,0:T(8,128)S(1)}, u32[]{:S(2)}, u32[]{:S(2)}) %collective-permute-start.13) | collective-permute-done | bytes 147488 | tf_op jit(solution)/shard_map/ppermute | solution.py:257
  103.9 2.8 %collective-permute-done.15.refs_3_ = f32[6,48,128]{2,1,0:T(8,128)S(1)} collective-permute-done((f32[6,48,128]{2,1,0:T(8,128)S(1)}, f32[6,48,128]{2,1,0:T(8,128)S(1)}, u32[]{:S(2)}, u32[]{:S(2)}) %collective-permute-start.15) | collective-permute-done | bytes 147488 | tf_op jit(solution)/shard_map/ppermute | solution.py:257
  (61 shorter events, 21.3 us)
Async XLA Ops:
  3.2 6.7 %collective-permute-start.25 = (f32[72,256]{1,0:T(8,128)S(1)}, f32[72,256]{1,0:T(8,128)S(1)}, u32[]{:S(2)}, u32[]{:S(2)}) collective-permute-start(f32[72,256]{1,0:T(8,128)S(1)} %get-tuple-element.92), channel_id=1, source_target_pairs={{0,4},{4,0},{8,12},{12,8},{16,20},{20,16},{24,28},{28,24},{1,5},{5... | collective-permute-start | bytes 221192 | tf_op jit(solution)/shard_map/ppermute | solution.py:257
  3.7 6.8 %collective-permute-start.27 = (f32[72,256]{1,0:T(8,128)S(1)}, f32[72,256]{1,0:T(8,128)S(1)}, u32[]{:S(2)}, u32[]{:S(2)}) collective-permute-start(f32[72,256]{1,0:T(8,128)S(1)} %get-tuple-element.94), channel_id=1, source_target_pairs={{0,12},{4,8},{8,4},{12,0},{16,28},{20,24},{24,20},{28,16},{1,13},{... | collective-permute-start | bytes 221192 | tf_op jit(solution)/shard_map/ppermute | solution.py:257
  5.7 11.9 %collective-permute-start.16 = (f32[288,128]{1,0:T(8,128)S(1)}, f32[288,128]{1,0:T(8,128)S(1)}, u32[]{:S(2)}, u32[]{:S(2)}) collective-permute-start(f32[288,128]{1,0:T(8,128)S(1)} %get-tuple-element.80), channel_id=1, source_target_pairs={{0,1},{1,0},{2,3},{3,2},{4,5},{5,4},{6,7},{7,6},{8,9},{9,8},{10,11... | collective-permute-start | bytes 442376 | tf_op jit(solution)/shard_map/ppermute | solution.py:257
  7.3 7.4 %collective-permute-start.28 = (f32[72,256]{1,0:T(8,128)S(1)}, f32[72,256]{1,0:T(8,128)S(1)}, u32[]{:S(2)}, u32[]{:S(2)}) collective-permute-start(f32[72,256]{1,0:T(8,128)S(1)} %get-tuple-element.95), channel_id=1, source_target_pairs={{0,16},{4,20},{8,24},{12,28},{16,0},{20,4},{24,8},{28,12},{1,17},{... | collective-permute-start | bytes 221192 | tf_op jit(solution)/shard_map/ppermute | solution.py:257
  9.9 32.2 %collective-permute-start.1 = (f32[576,128]{1,0:T(8,128)S(1)}, f32[576,128]{1,0:T(8,128)S(1)}, u32[]{:S(2)}, u32[]{:S(2)}) collective-permute-start(f32[576,128]{1,0:T(8,128)S(1)} %get-tuple-element.59), channel_id=1, source_target_pairs={{0,1},{1,0},{2,3},{3,2},{4,5},{5,4},{6,7},{7,6},{8,9},{9,8},{10,11... | collective-permute-start | bytes 884744 | tf_op jit(solution)/shard_map/ppermute | solution.py:257
  10.5 33.1 %collective-permute-start.2 = (f32[576,128]{1,0:T(8,128)S(1)}, f32[576,128]{1,0:T(8,128)S(1)}, u32[]{:S(2)}, u32[]{:S(2)}) collective-permute-start(f32[576,128]{1,0:T(8,128)S(1)} %get-tuple-element.60), channel_id=1, source_target_pairs={{0,2},{1,3},{2,0},{3,1},{4,6},{5,7},{6,4},{7,5},{8,10},{9,11},{10,... | collective-permute-start | bytes 884744 | tf_op jit(solution)/shard_map/ppermute | solution.py:257
  14.6 17.5 %collective-permute-start.17 = (f32[288,128]{1,0:T(8,128)S(1)}, f32[288,128]{1,0:T(8,128)S(1)}, u32[]{:S(2)}, u32[]{:S(2)}) collective-permute-start(f32[288,128]{1,0:T(8,128)S(1)} %get-tuple-element.81), channel_id=1, source_target_pairs={{0,2},{1,3},{2,0},{3,1},{4,6},{5,7},{6,4},{7,5},{8,10},{9,11},{10,... | collective-permute-start | bytes 442376 | tf_op jit(solution)/shard_map/ppermute | solution.py:257
  16.2 17.5 %collective-permute-start.18 = (f32[288,128]{1,0:T(8,128)S(1)}, f32[288,128]{1,0:T(8,128)S(1)}, u32[]{:S(2)}, u32[]{:S(2)}) collective-permute-start(f32[288,128]{1,0:T(8,128)S(1)} %get-tuple-element.82), channel_id=1, source_target_pairs={{0,3},{1,2},{2,1},{3,0},{4,7},{5,6},{6,5},{7,4},{8,11},{9,10},{10,... | collective-permute-start | bytes 442376 | tf_op jit(solution)/shard_map/ppermute | solution.py:257
  17.6 26.4 %collective-permute-start.3 = (f32[576,128]{1,0:T(8,128)S(1)}, f32[576,128]{1,0:T(8,128)S(1)}, u32[]{:S(2)}, u32[]{:S(2)}) collective-permute-start(f32[576,128]{1,0:T(8,128)S(1)} %get-tuple-element.61), channel_id=1, source_target_pairs={{0,3},{1,2},{2,1},{3,0},{4,7},{5,6},{6,5},{7,4},{8,11},{9,10},{10,... | collective-permute-start | bytes 884744 | tf_op jit(solution)/shard_map/ppermute | solution.py:257
  32.1 6.7 %collective-permute-start.30 = (f32[72,256]{1,0:T(8,128)S(1)}, f32[72,256]{1,0:T(8,128)S(1)}, u32[]{:S(2)}, u32[]{:S(2)}) collective-permute-start(f32[72,256]{1,0:T(8,128)S(1)} %get-tuple-element.97), channel_id=1, source_target_pairs={{0,24},{4,28},{8,16},{12,20},{16,8},{20,12},{24,0},{28,4},{1,25},{... | collective-permute-start | bytes 221192 | tf_op jit(solution)/shard_map/ppermute | solution.py:257
  38.8 14.0 %collective-permute-start.19 = (f32[288,128]{1,0:T(8,128)S(1)}, f32[288,128]{1,0:T(8,128)S(1)}, u32[]{:S(2)}, u32[]{:S(2)}) collective-permute-start(f32[288,128]{1,0:T(8,128)S(1)} %get-tuple-element.84), channel_id=1, source_target_pairs={{0,8},{4,12},{8,0},{12,4},{16,24},{20,28},{24,16},{28,20},{1,9},{5... | collective-permute-start | bytes 442376 | tf_op jit(solution)/shard_map/ppermute | solution.py:257
  42.0 7.4 %collective-permute-start.33 = (f32[216,128]{1,0:T(8,128)S(1)}, f32[216,128]{1,0:T(8,128)S(1)}, u32[]{:S(2)}, u32[]{:S(2)}) collective-permute-start(f32[216,128]{1,0:T(8,128)S(1)} %get-tuple-element.101), channel_id=1, source_target_pairs={{0,2},{1,3},{2,0},{3,1},{4,6},{5,7},{6,4},{7,5},{8,10},{9,11},{10,... | collective-permute-start | bytes 331784 | tf_op jit(solution)/shard_map/ppermute | solution.py:257
  44.0 12.7 %collective-permute-start.20 = (f32[288,128]{1,0:T(8,128)S(1)}, f32[288,128]{1,0:T(8,128)S(1)}, u32[]{:S(2)}, u32[]{:S(2)}) collective-permute-start(f32[288,128]{1,0:T(8,128)S(1)} %get-tuple-element.85), channel_id=1, source_target_pairs={{0,16},{4,20},{8,24},{12,28},{16,0},{20,4},{24,8},{28,12},{1,17},{... | collective-permute-start | bytes 442376 | tf_op jit(solution)/shard_map/ppermute | solution.py:257
  46.9 19.2 %collective-permute-start.21 = (f32[288,128]{1,0:T(8,128)S(1)}, f32[288,128]{1,0:T(8,128)S(1)}, u32[]{:S(2)}, u32[]{:S(2)}) collective-permute-start(f32[288,128]{1,0:T(8,128)S(1)} %get-tuple-element.86), channel_id=1, source_target_pairs={{0,24},{4,28},{8,16},{12,20},{16,8},{20,12},{24,0},{28,4},{1,25},{... | collective-permute-start | bytes 442376 | tf_op jit(solution)/shard_map/ppermute | solution.py:257
  49.5 18.1 %collective-permute-start.10 = (f32[288,128]{1,0:T(8,128)S(1)}, f32[288,128]{1,0:T(8,128)S(1)}, u32[]{:S(2)}, u32[]{:S(2)}) collective-permute-start(f32[288,128]{1,0:T(8,128)S(1)} %get-tuple-element.72), channel_id=1, source_target_pairs={{0,8},{4,12},{8,0},{12,4},{16,24},{20,28},{24,16},{28,20},{1,9},{5... | collective-permute-start | bytes 442376 | tf_op jit(solution)/shard_map/ppermute | solution.py:257
  50.0 18.7 %collective-permute-start.11 = (f32[288,128]{1,0:T(8,128)S(1)}, f32[288,128]{1,0:T(8,128)S(1)}, u32[]{:S(2)}, u32[]{:S(2)}) collective-permute-start(f32[288,128]{1,0:T(8,128)S(1)} %get-tuple-element.73), channel_id=1, source_target_pairs={{0,16},{4,20},{8,24},{12,28},{16,0},{20,4},{24,8},{28,12},{1,17},{... | collective-permute-start | bytes 442376 | tf_op jit(solution)/shard_map/ppermute | solution.py:257
  52.8 20.4 %collective-permute-start.12 = (f32[288,128]{1,0:T(8,128)S(1)}, f32[288,128]{1,0:T(8,128)S(1)}, u32[]{:S(2)}, u32[]{:S(2)}) collective-permute-start(f32[288,128]{1,0:T(8,128)S(1)} %get-tuple-element.74), channel_id=1, source_target_pairs={{0,24},{4,28},{8,16},{12,20},{16,8},{20,12},{24,0},{28,4},{1,25},{... | collective-permute-start | bytes 442376 | tf_op jit(solution)/shard_map/ppermute | solution.py:257
  56.7 26.8 %collective-permute-start.35 = (f32[6,48,128]{2,1,0:T(8,128)S(1)}, f32[6,48,128]{2,1,0:T(8,128)S(1)}, u32[]{:S(2)}, u32[]{:S(2)}) collective-permute-start(f32[6,48,128]{2,1,0:T(8,128)S(1)} %get-tuple-element.104), channel_id=1, source_target_pairs={{0,1},{1,0},{2,3},{3,2},{4,5},{5,4},{6,7},{7,6},{8,9},{9,8},{10,11... | collective-permute-start | bytes 442376 | tf_op jit(solution)/shard_map/ppermute | solution.py:257
  66.1 20.1 %collective-permute-start.36 = (f32[6,48,128]{2,1,0:T(8,128)S(1)}, f32[6,48,128]{2,1,0:T(8,128)S(1)}, u32[]{:S(2)}, u32[]{:S(2)}) collective-permute-start(f32[6,48,128]{2,1,0:T(8,128)S(1)} %get-tuple-element.105), channel_id=1, source_target_pairs={{0,2},{1,3},{2,0},{3,1},{4,6},{5,7},{6,4},{7,5},{8,10},{9,11},{10,... | collective-permute-start | bytes 442376 | tf_op jit(solution)/shard_map/ppermute | solution.py:257
  67.6 19.1 %collective-permute-start.4 = (f32[288,128]{1,0:T(8,128)S(1)}, f32[288,128]{1,0:T(8,128)S(1)}, u32[]{:S(2)}, u32[]{:S(2)}) collective-permute-start(f32[288,128]{1,0:T(8,128)S(1)} %get-tuple-element.63), channel_id=1, source_target_pairs={{0,8},{4,12},{8,0},{12,4},{16,24},{20,28},{24,16},{28,20},{1,9},{5... | collective-permute-start | bytes 442376 | tf_op jit(solution)/shard_map/ppermute | solution.py:257
  68.7 18.4 %collective-permute-start.5 = (f32[288,128]{1,0:T(8,128)S(1)}, f32[288,128]{1,0:T(8,128)S(1)}, u32[]{:S(2)}, u32[]{:S(2)}) collective-permute-start(f32[288,128]{1,0:T(8,128)S(1)} %get-tuple-element.64), channel_id=1, source_target_pairs={{0,16},{4,20},{8,24},{12,28},{16,0},{20,4},{24,8},{28,12},{1,17},{... | collective-permute-start | bytes 442376 | tf_op jit(solution)/shard_map/ppermute | solution.py:257
  73.2 16.4 %collective-permute-start.6 = (f32[288,128]{1,0:T(8,128)S(1)}, f32[288,128]{1,0:T(8,128)S(1)}, u32[]{:S(2)}, u32[]{:S(2)}) collective-permute-start(f32[288,128]{1,0:T(8,128)S(1)} %get-tuple-element.65), channel_id=1, source_target_pairs={{0,24},{4,28},{8,16},{12,20},{16,8},{20,12},{24,0},{28,4},{1,25},{... | collective-permute-start | bytes 442376 | tf_op jit(solution)/shard_map/ppermute | solution.py:257
  83.6 8.3 %collective-permute-start.37 = (f32[6,48,128]{2,1,0:T(8,128)S(1)}, f32[6,48,128]{2,1,0:T(8,128)S(1)}, u32[]{:S(2)}, u32[]{:S(2)}) collective-permute-start(f32[6,48,128]{2,1,0:T(8,128)S(1)} %get-tuple-element.106), channel_id=1, source_target_pairs={{0,3},{1,2},{2,1},{3,0},{4,7},{5,6},{6,5},{7,4},{8,11},{9,10},{10,... | collective-permute-start | bytes 442376 | tf_op jit(solution)/shard_map/ppermute | solution.py:257
  86.2 8.3 %collective-permute-start.22 = (f32[6,48,128]{2,1,0:T(8,128)S(1)}, f32[6,48,128]{2,1,0:T(8,128)S(1)}, u32[]{:S(2)}, u32[]{:S(2)}) collective-permute-start(f32[6,48,128]{2,1,0:T(8,128)S(1)} %get-tuple-element.88), channel_id=1, source_target_pairs={{0,1},{1,0},{2,3},{3,2},{4,5},{5,4},{6,7},{7,6},{8,9},{9,8},{10,11... | collective-permute-start | bytes 442376 | tf_op jit(solution)/shard_map/ppermute | solution.py:257
  86.6 8.4 %collective-permute-start.23 = (f32[6,48,128]{2,1,0:T(8,128)S(1)}, f32[6,48,128]{2,1,0:T(8,128)S(1)}, u32[]{:S(2)}, u32[]{:S(2)}) collective-permute-start(f32[6,48,128]{2,1,0:T(8,128)S(1)} %get-tuple-element.89), channel_id=1, source_target_pairs={{0,2},{1,3},{2,0},{3,1},{4,6},{5,7},{6,4},{7,5},{8,10},{9,11},{10,... | collective-permute-start | bytes 442376 | tf_op jit(solution)/shard_map/ppermute | solution.py:257
  87.1 10.8 %collective-permute-start.24 = (f32[6,48,128]{2,1,0:T(8,128)S(1)}, f32[6,48,128]{2,1,0:T(8,128)S(1)}, u32[]{:S(2)}, u32[]{:S(2)}) collective-permute-start(f32[6,48,128]{2,1,0:T(8,128)S(1)} %get-tuple-element.90), channel_id=1, source_target_pairs={{0,3},{1,2},{2,1},{3,0},{4,7},{5,6},{6,5},{7,4},{8,11},{9,10},{10,... | collective-permute-start | bytes 442376 | tf_op jit(solution)/shard_map/ppermute | solution.py:257
  89.7 11.1 %collective-permute-start.13 = (f32[6,48,128]{2,1,0:T(8,128)S(1)}, f32[6,48,128]{2,1,0:T(8,128)S(1)}, u32[]{:S(2)}, u32[]{:S(2)}) collective-permute-start(f32[6,48,128]{2,1,0:T(8,128)S(1)} %get-tuple-element.76), channel_id=1, source_target_pairs={{0,1},{1,0},{2,3},{3,2},{4,5},{5,4},{6,7},{7,6},{8,9},{9,8},{10,11... | collective-permute-start | bytes 442376 | tf_op jit(solution)/shard_map/ppermute | solution.py:257
  91.8 15.9 %collective-permute-start.7 = (f32[6,48,128]{2,1,0:T(8,128)S(1)}, f32[6,48,128]{2,1,0:T(8,128)S(1)}, u32[]{:S(2)}, u32[]{:S(2)}) collective-permute-start(f32[6,48,128]{2,1,0:T(8,128)S(1)} %get-tuple-element.68), channel_id=1, source_target_pairs={{0,1},{1,0},{2,3},{3,2},{4,5},{5,4},{6,7},{7,6},{8,9},{9,8},{10,11... | collective-permute-start | bytes 442376 | tf_op jit(solution)/shard_map/ppermute | solution.py:257
  94.5 9.4 %collective-permute-start.14 = (f32[6,48,128]{2,1,0:T(8,128)S(1)}, f32[6,48,128]{2,1,0:T(8,128)S(1)}, u32[]{:S(2)}, u32[]{:S(2)}) collective-permute-start(f32[6,48,128]{2,1,0:T(8,128)S(1)} %get-tuple-element.77), channel_id=1, source_target_pairs={{0,2},{1,3},{2,0},{3,1},{4,6},{5,7},{6,4},{7,5},{8,10},{9,11},{10,... | collective-permute-start | bytes 442376 | tf_op jit(solution)/shard_map/ppermute | solution.py:257
  95.0 11.6 %collective-permute-start.15 = (f32[6,48,128]{2,1,0:T(8,128)S(1)}, f32[6,48,128]{2,1,0:T(8,128)S(1)}, u32[]{:S(2)}, u32[]{:S(2)}) collective-permute-start(f32[6,48,128]{2,1,0:T(8,128)S(1)} %get-tuple-element.78), channel_id=1, source_target_pairs={{0,3},{1,2},{2,1},{3,0},{4,7},{5,6},{6,5},{7,4},{8,11},{9,10},{10,... | collective-permute-start | bytes 442376 | tf_op jit(solution)/shard_map/ppermute | solution.py:257
  97.9 10.7 %collective-permute-start.8 = (f32[6,48,128]{2,1,0:T(8,128)S(1)}, f32[6,48,128]{2,1,0:T(8,128)S(1)}, u32[]{:S(2)}, u32[]{:S(2)}) collective-permute-start(f32[6,48,128]{2,1,0:T(8,128)S(1)} %get-tuple-element.69), channel_id=1, source_target_pairs={{0,2},{1,3},{2,0},{3,1},{4,6},{5,7},{6,4},{7,5},{8,10},{9,11},{10,... | collective-permute-start | bytes 442376 | tf_op jit(solution)/shard_map/ppermute | solution.py:257
  100.8 7.8 %collective-permute-start.9 = (f32[6,48,128]{2,1,0:T(8,128)S(1)}, f32[6,48,128]{2,1,0:T(8,128)S(1)}, u32[]{:S(2)}, u32[]{:S(2)}) collective-permute-start(f32[6,48,128]{2,1,0:T(8,128)S(1)} %get-tuple-element.70), channel_id=1, source_target_pairs={{0,3},{1,2},{2,1},{3,0},{4,7},{5,6},{6,5},{7,4},{8,11},{9,10},{10,... | collective-permute-start | bytes 442376 | tf_op jit(solution)/shard_map/ppermute | solution.py:257
  (7 other events, 36.2 us)
where the time goes:
time: 110 us
  starting transfers between devices  52.9 us (48%)
  waiting for transfers between devices  42.7 us (39%)
  Pallas kernels  12.1 us (11%)
  local copies, waits for them, and re-layouts  1.89 us (2%)
    ppermute x38, starting transfers between devices, swap(): lax.ppermute(x, axis, [(i, i ^ k) for i in range(lax.axis_size(axis))])  52.9 us
    ppermute x38, waiting for transfers between devices, swap(): lax.ppermute(x, axis, [(i, i ^ k) for i in range(lax.axis_size(axis))])  42.7 us
    pallas_call x11, Pallas kernels, call(): pl.pallas_call(kernel, out_shape=[jax.ShapeDtypeStruct(o, jnp.float32) fo...  7.81 us
    pallas_call x4, Pallas kernels, per_device(): pl.pallas_call(functools.partial(place_kernel, groups), out_shape=jax.Sha...  4.32 us
  transfers between devices with their start and end apart: 38, of which 14 were waited for; matrix products, arithmetic and copies ran while one was open for 0% of the time, Pallas kernels for 9%

commit v1 on v0

--- a/solution.py
+++ b/solution.py
@@ -14,6 +14,7 @@
 PART = LANES // FOLD
 YEAR = 12
 VMEM_LIMIT = 48 * 1024 * 1024
+PACK_LIMIT = 50 * 1024 * 1024
 
 
 def low_lanes(rows):
@@ -25,7 +26,8 @@
 
 
 def pack_kernel(tm, halves, groups, block, width, chunks, x_ref, *refs):
-    first_refs, kept_ref, other_ref, held = refs[:tm], refs[tm], refs[tm + 1], refs[tm + 2]
+    first_refs, kept_ref, other_ref = refs[:tm], refs[tm], refs[tm + 1]
+    held, own, sems = refs[tm + 2 :]
     me = lax.axis_index("tm")
     at_group = lax.axis_index("member")
     members, months = x_ref.shape[0], x_ref.shape[1]
@@ -34,25 +36,35 @@
     low = low_lanes(rows)
 
     def rows_of(k, lane, times):
-        lanes = pl.ds(pl.multiple_of((me ^ k) * block + lane, LANES), LANES)
-        return jnp.concatenate([x_ref[:, t, lanes] for t in times], axis=0)
+        lanes = slice(lane, lane + LANES)
+        return jnp.concatenate([own[k, :, t, lanes] for t in times], axis=0)
+
+    def copy(k):
+        lanes = pl.ds(pl.multiple_of((me ^ k) * block, LANES), block)
+        return pltpu.make_async_copy(x_ref.at[:, :, lanes], own.at[k], sems.at[k])
 
     for k in range(tm):
+        copy(k).start()
+    size = (tm // halves) * rows
+    for k in range(tm):
+        copy(k).wait()
         for lane in range(0, width, LANES):
             first_refs[k][:, lane : lane + LANES] = rows_of(k, lane, range(months))
-    size = (tm // halves) * rows
-    for c in range(1, chunks):
-        for h, out_ref in enumerate((kept_ref, other_ref)):
-            for y in range(tm // halves):
-                at_rows = slice(y * rows, (y + 1) * rows)
-                for p in range(groups // FOLD):
-                    lane = c * width + p * LANES
-                    a = rows_of(y * halves + h, lane, range(steps))
-                    b = rows_of(y * halves + h, lane, range(steps, months))
-                    held[FOLD * p, at_rows, :], held[FOLD * p + 1, at_rows, :] = split_lanes(a, b, low)
+        y, h = divmod(k, halves)
+        at_rows = slice(y * rows, (y + 1) * rows)
+        for c in range(1, chunks):
+            at = h * (chunks - 1) + c - 1
+            for p in range(groups // FOLD):
+                lane = c * width + p * LANES
+                a = rows_of(k, lane, range(steps))
+                b = rows_of(k, lane, range(steps, months))
+                a, b = split_lanes(a, b, low)
+                held[at, FOLD * p, at_rows, :], held[at, FOLD * p + 1, at_rows, :] = a, b
+    for h, out_ref in enumerate((kept_ref, other_ref)):
+        for c in range(1, chunks):
             for d in range(groups):
                 row = ((c - 1) * groups + d) * size
-                out_ref[row : row + size, :] = held[at_group ^ d]
+                out_ref[row : row + size, :] = held[h * (chunks - 1) + c - 1, at_group ^ d]
 
 
 def merge_kernel(groups, sets, kept_ref, other_ref, *out_refs):
@@ -285,16 +297,26 @@
     assert halves == 2 and months % FOLD == 0 and members % FOLD == 0 and block == chunks * width
 
     both = ((chunks - 1) * groups * years * part_rows, LANES)
-    packed = call(
+    packed = pl.pallas_call(
         functools.partial(pack_kernel, tm, halves, groups, block, width, chunks),
-        [(rows, width)] * tm + [both] * 2, 4e6, fields,
-        scratch=[(groups, years * part_rows, LANES)],
-    )
+        out_shape=[jax.ShapeDtypeStruct((rows, width), jnp.float32)] * tm
+        + [jax.ShapeDtypeStruct(both, jnp.float32)] * 2,
+        in_specs=[pl.BlockSpec(memory_space=pl.ANY)],
+        out_specs=[pl.BlockSpec(memory_space=pltpu.VMEM)] * (tm + 2),
+        scratch_shapes=[
+            pltpu.VMEM((halves * (chunks - 1), groups, years * part_rows, LANES), jnp.float32),
+            pltpu.VMEM((tm, members, months, block), jnp.float32),
+            pltpu.SemaphoreType.DMA((tm,)),
+        ],
+        compiler_params=pltpu.CompilerParams(vmem_limit_bytes=PACK_LIMIT),
+        cost_estimate=pl.CostEstimate(flops=4000000, bytes_accessed=8 * fields.size, transcendentals=0),
+        name="pack",
+    )(fields)
     by_block, kept, other = packed[:tm], packed[tm], packed[tm + 1]
     other = swap(other, "tm", 1)
     arrived = {0: by_block[0]}
     for k in sorted(range(1, tm), key=lambda k: (-(k // halves), k)):
-        far = k >= tm - halves
+        far = k >= tm - halves or k == tm - halves - 1
         arrived[k] = swap(by_block[k], "tm", k)
     arrived = [arrived[k] for k in range(tm)]
 

time: 110 us -> 109 us (level)
  local copies, waits for them, and re-layouts: 1.89 us -> 0 us
  Pallas kernels: 12.1 us -> 13.5 us
    pallas_call x0 -> x1, Pallas kernels: none -> 2.61 us  [per_device(): pl.pallas_call(functools.partial(pack_kernel, tm, halves, groups, block,...]
    unnamed x2 -> x0, local copies, waits for them, and re-layouts: 1.89 us -> none
    pallas_call x11 -> x10, Pallas kernels: 7.81 us -> 6.6 us  [call(): pl.pallas_call(kernel, out_shape=[jax.ShapeDtypeStruct(o, jnp.float32) fo...]
where the time goes in v1:
time: 109 us
  starting transfers between devices  52.9 us (49%)
  waiting for transfers between devices  42.7 us (39%)
  Pallas kernels  13.5 us (12%)
    ppermute x38, starting transfers between devices, swap(): lax.ppermute(x, axis, [(i, i ^ k) for i in range(lax.axis_size(axis))])  52.9 us
    ppermute x38, waiting for transfers between devices, swap(): lax.ppermute(x, axis, [(i, i ^ k) for i in range(lax.axis_size(axis))])  42.7 us
    pallas_call x10, Pallas kernels, call(): pl.pallas_call(kernel, out_shape=[jax.ShapeDtypeStruct(o, jnp.float32) fo...  6.6 us
    pallas_call x4, Pallas kernels, per_device(): pl.pallas_call(functools.partial(place_kernel, groups), out_shape=jax.Sha...  4.32 us
    pallas_call x1, Pallas kernels, per_device(): pl.pallas_call(functools.partial(pack_kernel, tm, halves, groups, block,...  2.61 us
  transfers between devices with their start and end apart: 38, of which 14 were waited for; matrix products, arithmetic and copies ran while one was open for 0% of the time, Pallas kernels for 9%

profile of v1, /device:TPU:8, one launch (start us, length us, event | category | flops | bytes accessed | tf_op | source)
XLA Modules:
  0.0 109.2 jit_solution(1927788154695741015)
XLA Ops:
  0.0 2.6 %pack.1 = (f32[72,256]{1,0:T(8,128)S(1)}, f32[72,256]{1,0:T(8,128)S(1)}, f32[72,256]{1,0:T(8,128)S(1)}, f32[72,256]{1,0:T(8,128)S(1)}, f32[72,256]{1,0:T(8,128)S...) custom-call(f32[12,6,8192]{2,1,0:T(8,128)} %x_ref.1), custom_call_target="tpu_custom_call" | custom-call | flops 4000000 | bytes 4718592 | tf_op jit(solution)/shard_map/pack/pallas_call | solution.py:300
  3.2 1.4 %collective-permute-start.27 = (f32[72,256]{1,0:T(8,128)S(1)}, f32[72,256]{1,0:T(8,128)S(1)}, u32[]{:S(2)}, u32[]{:S(2)}) collective-permute-start(f32[72,256]{1,0:T(8,128)S(1)} %get-tuple-element.94), channel_id=1, source_target_pairs={{0,12},{4,8},{8,4},{12,0},{16,28},{20,24},{24,20},{28,16},{1,13},{... | collective-permute-start | bytes 221192 | tf_op jit(solution)/shard_map/ppermute | solution.py:269
  5.2 1.6 %collective-permute-start.16 = (f32[288,128]{1,0:T(8,128)S(1)}, f32[288,128]{1,0:T(8,128)S(1)}, u32[]{:S(2)}, u32[]{:S(2)}) collective-permute-start(f32[288,128]{1,0:T(8,128)S(1)} %get-tuple-element.80), channel_id=1, source_target_pairs={{0,1},{1,0},{2,3},{3,2},{4,5},{5,4},{6,7},{7,6},{8,9},{9,8},{10,11... | collective-permute-start | bytes 442376 | tf_op jit(solution)/shard_map/ppermute | solution.py:269
  6.8 2.6 %collective-permute-start.28 = (f32[72,256]{1,0:T(8,128)S(1)}, f32[72,256]{1,0:T(8,128)S(1)}, u32[]{:S(2)}, u32[]{:S(2)}) collective-permute-start(f32[72,256]{1,0:T(8,128)S(1)} %get-tuple-element.95), channel_id=1, source_target_pairs={{0,16},{4,20},{8,24},{12,28},{16,0},{20,4},{24,8},{28,12},{1,17},{... | collective-permute-start | bytes 221192 | tf_op jit(solution)/shard_map/ppermute | solution.py:269
  10.0 1.5 %collective-permute-start.2 = (f32[576,128]{1,0:T(8,128)S(1)}, f32[576,128]{1,0:T(8,128)S(1)}, u32[]{:S(2)}, u32[]{:S(2)}) collective-permute-start(f32[576,128]{1,0:T(8,128)S(1)} %get-tuple-element.60), channel_id=1, source_target_pairs={{0,2},{1,3},{2,0},{3,1},{4,6},{5,7},{6,4},{7,5},{8,10},{9,11},{10,... | collective-permute-start | bytes 884744 | tf_op jit(solution)/shard_map/ppermute | solution.py:269
  11.5 2.6 %collective-permute-done.28.refs_4_ = f32[72,256]{1,0:T(8,128)S(1)} collective-permute-done((f32[72,256]{1,0:T(8,128)S(1)}, f32[72,256]{1,0:T(8,128)S(1)}, u32[]{:S(2)}, u32[]{:S(2)}) %collective-permute-start.28) | collective-permute-done | bytes 73760 | tf_op jit(solution)/shard_map/ppermute | solution.py:269
  14.2 1.5 %collective-permute-start.17 = (f32[288,128]{1,0:T(8,128)S(1)}, f32[288,128]{1,0:T(8,128)S(1)}, u32[]{:S(2)}, u32[]{:S(2)}) collective-permute-start(f32[288,128]{1,0:T(8,128)S(1)} %get-tuple-element.81), channel_id=1, source_target_pairs={{0,2},{1,3},{2,0},{3,1},{4,6},{5,7},{6,4},{7,5},{8,10},{9,11},{10,... | collective-permute-start | bytes 442376 | tf_op jit(solution)/shard_map/ppermute | solution.py:269
  15.7 1.5 %collective-permute-start.18 = (f32[288,128]{1,0:T(8,128)S(1)}, f32[288,128]{1,0:T(8,128)S(1)}, u32[]{:S(2)}, u32[]{:S(2)}) collective-permute-start(f32[288,128]{1,0:T(8,128)S(1)} %get-tuple-element.82), channel_id=1, source_target_pairs={{0,3},{1,2},{2,1},{3,0},{4,7},{5,6},{6,5},{7,4},{8,11},{9,10},{10,... | collective-permute-start | bytes 442376 | tf_op jit(solution)/shard_map/ppermute | solution.py:269
  17.1 1.5 %collective-permute-start.3 = (f32[576,128]{1,0:T(8,128)S(1)}, f32[576,128]{1,0:T(8,128)S(1)}, u32[]{:S(2)}, u32[]{:S(2)}) collective-permute-start(f32[576,128]{1,0:T(8,128)S(1)} %get-tuple-element.61), channel_id=1, source_target_pairs={{0,3},{1,2},{2,1},{3,0},{4,7},{5,6},{6,5},{7,4},{8,11},{9,10},{10,... | collective-permute-start | bytes 884744 | tf_op jit(solution)/shard_map/ppermute | solution.py:269
  18.6 13.0 %collective-permute-done.17.refs_2_ = f32[288,128]{1,0:T(8,128)S(1)} collective-permute-done((f32[288,128]{1,0:T(8,128)S(1)}, f32[288,128]{1,0:T(8,128)S(1)}, u32[]{:S(2)}, u32[]{:S(2)}) %collective-permute-start.17) | collective-permute-done | bytes 147488 | tf_op jit(solution)/shard_map/ppermute | solution.py:269
  31.6 1.6 %collective-permute-start.30 = (f32[72,256]{1,0:T(8,128)S(1)}, f32[72,256]{1,0:T(8,128)S(1)}, u32[]{:S(2)}, u32[]{:S(2)}) collective-permute-start(f32[72,256]{1,0:T(8,128)S(1)} %get-tuple-element.97), channel_id=1, source_target_pairs={{0,24},{4,28},{8,16},{12,20},{16,8},{20,12},{24,0},{28,4},{1,25},{... | collective-permute-start | bytes 221192 | tf_op jit(solution)/shard_map/ppermute | solution.py:269
  33.3 5.0 %collective-permute-done.30.refs_6_ = f32[72,256]{1,0:T(8,128)S(1)} collective-permute-done((f32[72,256]{1,0:T(8,128)S(1)}, f32[72,256]{1,0:T(8,128)S(1)}, u32[]{:S(2)}, u32[]{:S(2)}) %collective-permute-start.30) | collective-permute-done | bytes 73760 | tf_op jit(solution)/shard_map/ppermute | solution.py:269
  40.0 1.6 %collective-permute-start.32 = (f32[216,128]{1,0:T(8,128)S(1)}, f32[216,128]{1,0:T(8,128)S(1)}, u32[]{:S(2)}, u32[]{:S(2)}) collective-permute-start(f32[216,128]{1,0:T(8,128)S(1)} %get-tuple-element.100), channel_id=1, source_target_pairs={{0,1},{1,0},{2,3},{3,2},{4,5},{5,4},{6,7},{7,6},{8,9},{9,8},{10,11... | collective-permute-start | bytes 331784 | tf_op jit(solution)/shard_map/ppermute | solution.py:269
  41.5 1.5 %collective-permute-start.33 = (f32[216,128]{1,0:T(8,128)S(1)}, f32[216,128]{1,0:T(8,128)S(1)}, u32[]{:S(2)}, u32[]{:S(2)}) collective-permute-start(f32[216,128]{1,0:T(8,128)S(1)} %get-tuple-element.101), channel_id=1, source_target_pairs={{0,2},{1,3},{2,0},{3,1},{4,6},{5,7},{6,4},{7,5},{8,10},{9,11},{10,... | collective-permute-start | bytes 331784 | tf_op jit(solution)/shard_map/ppermute | solution.py:269
  43.6 2.7 %collective-permute-start.20 = (f32[288,128]{1,0:T(8,128)S(1)}, f32[288,128]{1,0:T(8,128)S(1)}, u32[]{:S(2)}, u32[]{:S(2)}) collective-permute-start(f32[288,128]{1,0:T(8,128)S(1)} %get-tuple-element.85), channel_id=1, source_target_pairs={{0,16},{4,20},{8,24},{12,28},{16,0},{20,4},{24,8},{28,12},{1,17},{... | collective-permute-start | bytes 442376 | tf_op jit(solution)/shard_map/ppermute | solution.py:269
  47.3 1.7 %collective-permute-done.33.refs_2_ = f32[216,128]{1,0:T(8,128)S(1)} collective-permute-done((f32[216,128]{1,0:T(8,128)S(1)}, f32[216,128]{1,0:T(8,128)S(1)}, u32[]{:S(2)}, u32[]{:S(2)}) %collective-permute-start.33) | collective-permute-done | bytes 110624 | tf_op jit(solution)/shard_map/ppermute | solution.py:269
  49.5 2.8 %collective-permute-start.11 = (f32[288,128]{1,0:T(8,128)S(1)}, f32[288,128]{1,0:T(8,128)S(1)}, u32[]{:S(2)}, u32[]{:S(2)}) collective-permute-start(f32[288,128]{1,0:T(8,128)S(1)} %get-tuple-element.73), channel_id=1, source_target_pairs={{0,16},{4,20},{8,24},{12,28},{16,0},{20,4},{24,8},{28,12},{1,17},{... | collective-permute-start | bytes 442376 | tf_op jit(solution)/shard_map/ppermute | solution.py:269
  52.5 1.4 %shard_map.26 = (f32[6,48,128]{2,1,0:T(8,128)S(1)}, f32[6,48,128]{2,1,0:T(8,128)S(1)}, f32[6,48,128]{2,1,0:T(8,128)S(1)}, f32[6,48,128]{2,1,0:T(8,128)S(1)}) custom-call(f32[216,128]{1,0:T(8,128)S(1)} %get-tuple-element.99.refs_0_, f32[216,128]{1,0:T(8,128)S(1)} %collective-permute-done.32.refs_1_, f32[216,128]{1,0:T(8,128)S(1)} %collective-permute-done.33.refs_2_, ...), custom_call_target="tpu_custom_call" | custom-call | flops 10000000 | bytes 1032192 | tf_op jit(solution)/shard_map/pallas_call | solution.py:253
  53.9 2.3 %collective-permute-done.20.refs_2_ = f32[288,128]{1,0:T(8,128)S(1)} collective-permute-done((f32[288,128]{1,0:T(8,128)S(1)}, f32[288,128]{1,0:T(8,128)S(1)}, u32[]{:S(2)}, u32[]{:S(2)}) %collective-permute-start.20) | collective-permute-done | bytes 147488 | tf_op jit(solution)/shard_map/ppermute | solution.py:269
  56.3 1.9 %collective-permute-start.35 = (f32[6,48,128]{2,1,0:T(8,128)S(1)}, f32[6,48,128]{2,1,0:T(8,128)S(1)}, u32[]{:S(2)}, u32[]{:S(2)}) collective-permute-start(f32[6,48,128]{2,1,0:T(8,128)S(1)} %get-tuple-element.104), channel_id=1, source_target_pairs={{0,1},{1,0},{2,3},{3,2},{4,5},{5,4},{6,7},{7,6},{8,9},{9,8},{10,11... | collective-permute-start | bytes 442376 | tf_op jit(solution)/shard_map/ppermute | solution.py:269
  58.1 7.4 %collective-permute-done.21.refs_3_ = f32[288,128]{1,0:T(8,128)S(1)} collective-permute-done((f32[288,128]{1,0:T(8,128)S(1)}, f32[288,128]{1,0:T(8,128)S(1)}, u32[]{:S(2)}, u32[]{:S(2)}) %collective-permute-start.21) | collective-permute-done | bytes 147488 | tf_op jit(solution)/shard_map/ppermute | solution.py:269
  65.6 1.5 %collective-permute-start.36 = (f32[6,48,128]{2,1,0:T(8,128)S(1)}, f32[6,48,128]{2,1,0:T(8,128)S(1)}, u32[]{:S(2)}, u32[]{:S(2)}) collective-permute-start(f32[6,48,128]{2,1,0:T(8,128)S(1)} %get-tuple-element.105), channel_id=1, source_target_pairs={{0,2},{1,3},{2,0},{3,1},{4,6},{5,7},{6,4},{7,5},{8,10},{9,11},{10,... | collective-permute-start | bytes 442376 | tf_op jit(solution)/shard_map/ppermute | solution.py:269
  68.3 3.4 %collective-permute-start.5 = (f32[288,128]{1,0:T(8,128)S(1)}, f32[288,128]{1,0:T(8,128)S(1)}, u32[]{:S(2)}, u32[]{:S(2)}) collective-permute-start(f32[288,128]{1,0:T(8,128)S(1)} %get-tuple-element.64), channel_id=1, source_target_pairs={{0,16},{4,20},{8,24},{12,28},{16,0},{20,4},{24,8},{28,12},{1,17},{... | collective-permute-start | bytes 442376 | tf_op jit(solution)/shard_map/ppermute | solution.py:269
  72.7 7.5 %collective-permute-start.6 = (f32[288,128]{1,0:T(8,128)S(1)}, f32[288,128]{1,0:T(8,128)S(1)}, u32[]{:S(2)}, u32[]{:S(2)}) collective-permute-start(f32[288,128]{1,0:T(8,128)S(1)} %get-tuple-element.65), channel_id=1, source_target_pairs={{0,24},{4,28},{8,16},{12,20},{16,8},{20,12},{24,0},{28,4},{1,25},{... | collective-permute-start | bytes 442376 | tf_op jit(solution)/shard_map/ppermute | solution.py:269
  80.2 1.4 %shard_map.23 = (f32[6,48,128]{2,1,0:T(8,128)S(1)}, f32[6,48,128]{2,1,0:T(8,128)S(1)}, f32[6,48,128]{2,1,0:T(8,128)S(1)}, f32[6,48,128]{2,1,0:T(8,128)S(1)}) custom-call(f32[288,128]{1,0:T(8,128)S(1)} %get-tuple-element.83.refs_0_, f32[288,128]{1,0:T(8,128)S(1)} %collective-permute-done.19.refs_1_, f32[288,128]{1,0:T(8,128)S(1)} %collective-permute-done.20.refs_2_, ...), custom_call_target="tpu_custom_call" | custom-call | flops 10000000 | bytes 1179648 | tf_op jit(solution)/shard_map/pallas_call | solution.py:253
  81.6 1.4 %shard_map.21 = (f32[6,48,128]{2,1,0:T(8,128)S(1)}, f32[6,48,128]{2,1,0:T(8,128)S(1)}, f32[6,48,128]{2,1,0:T(8,128)S(1)}, f32[6,48,128]{2,1,0:T(8,128)S(1)}) custom-call(f32[288,128]{1,0:T(8,128)S(1)} %get-tuple-element.71.refs_0_, f32[288,128]{1,0:T(8,128)S(1)} %collective-permute-done.10.refs_1_, f32[288,128]{1,0:T(8,128)S(1)} %collective-permute-done.11.refs_2_, ...), custom_call_target="tpu_custom_call" | custom-call | flops 10000000 | bytes 1179648 | tf_op jit(solution)/shard_map/pallas_call | solution.py:253
  83.1 2.6 %collective-permute-start.37 = (f32[6,48,128]{2,1,0:T(8,128)S(1)}, f32[6,48,128]{2,1,0:T(8,128)S(1)}, u32[]{:S(2)}, u32[]{:S(2)}) collective-permute-start(f32[6,48,128]{2,1,0:T(8,128)S(1)} %get-tuple-element.106), channel_id=1, source_target_pairs={{0,3},{1,2},{2,1},{3,0},{4,7},{5,6},{6,5},{7,4},{8,11},{9,10},{10,... | collective-permute-start | bytes 442376 | tf_op jit(solution)/shard_map/ppermute | solution.py:269
  86.7 2.5 %collective-permute-start.24 = (f32[6,48,128]{2,1,0:T(8,128)S(1)}, f32[6,48,128]{2,1,0:T(8,128)S(1)}, u32[]{:S(2)}, u32[]{:S(2)}) collective-permute-start(f32[6,48,128]{2,1,0:T(8,128)S(1)} %get-tuple-element.90), channel_id=1, source_target_pairs={{0,3},{1,2},{2,1},{3,0},{4,7},{5,6},{6,5},{7,4},{8,11},{9,10},{10,... | collective-permute-start | bytes 442376 | tf_op jit(solution)/shard_map/ppermute | solution.py:269
  91.4 1.6 %collective-permute-start.7 = (f32[6,48,128]{2,1,0:T(8,128)S(1)}, f32[6,48,128]{2,1,0:T(8,128)S(1)}, u32[]{:S(2)}, u32[]{:S(2)}) collective-permute-start(f32[6,48,128]{2,1,0:T(8,128)S(1)} %get-tuple-element.68), channel_id=1, source_target_pairs={{0,1},{1,0},{2,3},{3,2},{4,5},{5,4},{6,7},{7,6},{8,9},{9,8},{10,11... | collective-permute-start | bytes 442376 | tf_op jit(solution)/shard_map/ppermute | solution.py:269
  94.5 2.9 %collective-permute-start.15 = (f32[6,48,128]{2,1,0:T(8,128)S(1)}, f32[6,48,128]{2,1,0:T(8,128)S(1)}, u32[]{:S(2)}, u32[]{:S(2)}) collective-permute-start(f32[6,48,128]{2,1,0:T(8,128)S(1)} %get-tuple-element.78), channel_id=1, source_target_pairs={{0,3},{1,2},{2,1},{3,0},{4,7},{5,6},{6,5},{7,4},{8,11},{9,10},{10,... | collective-permute-start | bytes 442376 | tf_op jit(solution)/shard_map/ppermute | solution.py:269
  98.6 1.7 %collective-permute-done.13.refs_1_ = f32[6,48,128]{2,1,0:T(8,128)S(1)} collective-permute-done((f32[6,48,128]{2,1,0:T(8,128)S(1)}, f32[6,48,128]{2,1,0:T(8,128)S(1)}, u32[]{:S(2)}, u32[]{:S(2)}) %collective-permute-start.13) | collective-permute-done | bytes 147488 | tf_op jit(solution)/shard_map/ppermute | solution.py:269
  103.4 2.8 %collective-permute-done.15.refs_3_ = f32[6,48,128]{2,1,0:T(8,128)S(1)} collective-permute-done((f32[6,48,128]{2,1,0:T(8,128)S(1)}, f32[6,48,128]{2,1,0:T(8,128)S(1)}, u32[]{:S(2)}, u32[]{:S(2)}) %collective-permute-start.15) | collective-permute-done | bytes 147488 | tf_op jit(solution)/shard_map/ppermute | solution.py:269
  (59 shorter events, 20.0 us)
Async XLA Ops:
  2.7 6.7 %collective-permute-start.25 = (f32[72,256]{1,0:T(8,128)S(1)}, f32[72,256]{1,0:T(8,128)S(1)}, u32[]{:S(2)}, u32[]{:S(2)}) collective-permute-start(f32[72,256]{1,0:T(8,128)S(1)} %get-tuple-element.92), channel_id=1, source_target_pairs={{0,4},{4,0},{8,12},{12,8},{16,20},{20,16},{24,28},{28,24},{1,5},{5... | collective-permute-start | bytes 221192 | tf_op jit(solution)/shard_map/ppermute | solution.py:269
  3.2 6.8 %collective-permute-start.27 = (f32[72,256]{1,0:T(8,128)S(1)}, f32[72,256]{1,0:T(8,128)S(1)}, u32[]{:S(2)}, u32[]{:S(2)}) collective-permute-start(f32[72,256]{1,0:T(8,128)S(1)} %get-tuple-element.94), channel_id=1, source_target_pairs={{0,12},{4,8},{8,4},{12,0},{16,28},{20,24},{24,20},{28,16},{1,13},{... | collective-permute-start | bytes 221192 | tf_op jit(solution)/shard_map/ppermute | solution.py:269
  5.2 11.9 %collective-permute-start.16 = (f32[288,128]{1,0:T(8,128)S(1)}, f32[288,128]{1,0:T(8,128)S(1)}, u32[]{:S(2)}, u32[]{:S(2)}) collective-permute-start(f32[288,128]{1,0:T(8,128)S(1)} %get-tuple-element.80), channel_id=1, source_target_pairs={{0,1},{1,0},{2,3},{3,2},{4,5},{5,4},{6,7},{7,6},{8,9},{9,8},{10,11... | collective-permute-start | bytes 442376 | tf_op jit(solution)/shard_map/ppermute | solution.py:269
  6.8 7.4 %collective-permute-start.28 = (f32[72,256]{1,0:T(8,128)S(1)}, f32[72,256]{1,0:T(8,128)S(1)}, u32[]{:S(2)}, u32[]{:S(2)}) collective-permute-start(f32[72,256]{1,0:T(8,128)S(1)} %get-tuple-element.95), channel_id=1, source_target_pairs={{0,16},{4,20},{8,24},{12,28},{16,0},{20,4},{24,8},{28,12},{1,17},{... | collective-permute-start | bytes 221192 | tf_op jit(solution)/shard_map/ppermute | solution.py:269
  9.4 32.2 %collective-permute-start.1 = (f32[576,128]{1,0:T(8,128)S(1)}, f32[576,128]{1,0:T(8,128)S(1)}, u32[]{:S(2)}, u32[]{:S(2)}) collective-permute-start(f32[576,128]{1,0:T(8,128)S(1)} %get-tuple-element.59), channel_id=1, source_target_pairs={{0,1},{1,0},{2,3},{3,2},{4,5},{5,4},{6,7},{7,6},{8,9},{9,8},{10,11... | collective-permute-start | bytes 884744 | tf_op jit(solution)/shard_map/ppermute | solution.py:269
  10.0 33.1 %collective-permute-start.2 = (f32[576,128]{1,0:T(8,128)S(1)}, f32[576,128]{1,0:T(8,128)S(1)}, u32[]{:S(2)}, u32[]{:S(2)}) collective-permute-start(f32[576,128]{1,0:T(8,128)S(1)} %get-tuple-element.60), channel_id=1, source_target_pairs={{0,2},{1,3},{2,0},{3,1},{4,6},{5,7},{6,4},{7,5},{8,10},{9,11},{10,... | collective-permute-start | bytes 884744 | tf_op jit(solution)/shard_map/ppermute | solution.py:269
  14.2 17.5 %collective-permute-start.17 = (f32[288,128]{1,0:T(8,128)S(1)}, f32[288,128]{1,0:T(8,128)S(1)}, u32[]{:S(2)}, u32[]{:S(2)}) collective-permute-start(f32[288,128]{1,0:T(8,128)S(1)} %get-tuple-element.81), channel_id=1, source_target_pairs={{0,2},{1,3},{2,0},{3,1},{4,6},{5,7},{6,4},{7,5},{8,10},{9,11},{10,... | collective-permute-start | bytes 442376 | tf_op jit(solution)/shard_map/ppermute | solution.py:269
  15.7 17.5 %collective-permute-start.18 = (f32[288,128]{1,0:T(8,128)S(1)}, f32[288,128]{1,0:T(8,128)S(1)}, u32[]{:S(2)}, u32[]{:S(2)}) collective-permute-start(f32[288,128]{1,0:T(8,128)S(1)} %get-tuple-element.82), channel_id=1, source_target_pairs={{0,3},{1,2},{2,1},{3,0},{4,7},{5,6},{6,5},{7,4},{8,11},{9,10},{10,... | collective-permute-start | bytes 442376 | tf_op jit(solution)/shard_map/ppermute | solution.py:269
  17.1 26.4 %collective-permute-start.3 = (f32[576,128]{1,0:T(8,128)S(1)}, f32[576,128]{1,0:T(8,128)S(1)}, u32[]{:S(2)}, u32[]{:S(2)}) collective-permute-start(f32[576,128]{1,0:T(8,128)S(1)} %get-tuple-element.61), channel_id=1, source_target_pairs={{0,3},{1,2},{2,1},{3,0},{4,7},{5,6},{6,5},{7,4},{8,11},{9,10},{10,... | collective-permute-start | bytes 884744 | tf_op jit(solution)/shard_map/ppermute | solution.py:269
  31.6 6.7 %collective-permute-start.30 = (f32[72,256]{1,0:T(8,128)S(1)}, f32[72,256]{1,0:T(8,128)S(1)}, u32[]{:S(2)}, u32[]{:S(2)}) collective-permute-start(f32[72,256]{1,0:T(8,128)S(1)} %get-tuple-element.97), channel_id=1, source_target_pairs={{0,24},{4,28},{8,16},{12,20},{16,8},{20,12},{24,0},{28,4},{1,25},{... | collective-permute-start | bytes 221192 | tf_op jit(solution)/shard_map/ppermute | solution.py:269
  38.3 14.0 %collective-permute-start.19 = (f32[288,128]{1,0:T(8,128)S(1)}, f32[288,128]{1,0:T(8,128)S(1)}, u32[]{:S(2)}, u32[]{:S(2)}) collective-permute-start(f32[288,128]{1,0:T(8,128)S(1)} %get-tuple-element.84), channel_id=1, source_target_pairs={{0,8},{4,12},{8,0},{12,4},{16,24},{20,28},{24,16},{28,20},{1,9},{5... | collective-permute-start | bytes 442376 | tf_op jit(solution)/shard_map/ppermute | solution.py:269
  41.5 7.4 %collective-permute-start.33 = (f32[216,128]{1,0:T(8,128)S(1)}, f32[216,128]{1,0:T(8,128)S(1)}, u32[]{:S(2)}, u32[]{:S(2)}) collective-permute-start(f32[216,128]{1,0:T(8,128)S(1)} %get-tuple-element.101), channel_id=1, source_target_pairs={{0,2},{1,3},{2,0},{3,1},{4,6},{5,7},{6,4},{7,5},{8,10},{9,11},{10,... | collective-permute-start | bytes 331784 | tf_op jit(solution)/shard_map/ppermute | solution.py:269
  43.6 12.7 %collective-permute-start.20 = (f32[288,128]{1,0:T(8,128)S(1)}, f32[288,128]{1,0:T(8,128)S(1)}, u32[]{:S(2)}, u32[]{:S(2)}) collective-permute-start(f32[288,128]{1,0:T(8,128)S(1)} %get-tuple-element.85), channel_id=1, source_target_pairs={{0,16},{4,20},{8,24},{12,28},{16,0},{20,4},{24,8},{28,12},{1,17},{... | collective-permute-start | bytes 442376 | tf_op jit(solution)/shard_map/ppermute | solution.py:269
  46.4 19.2 %collective-permute-start.21 = (f32[288,128]{1,0:T(8,128)S(1)}, f32[288,128]{1,0:T(8,128)S(1)}, u32[]{:S(2)}, u32[]{:S(2)}) collective-permute-start(f32[288,128]{1,0:T(8,128)S(1)} %get-tuple-element.86), channel_id=1, source_target_pairs={{0,24},{4,28},{8,16},{12,20},{16,8},{20,12},{24,0},{28,4},{1,25},{... | collective-permute-start | bytes 442376 | tf_op jit(solution)/shard_map/ppermute | solution.py:269
  49.0 18.1 %collective-permute-start.10 = (f32[288,128]{1,0:T(8,128)S(1)}, f32[288,128]{1,0:T(8,128)S(1)}, u32[]{:S(2)}, u32[]{:S(2)}) collective-permute-start(f32[288,128]{1,0:T(8,128)S(1)} %get-tuple-element.72), channel_id=1, source_target_pairs={{0,8},{4,12},{8,0},{12,4},{16,24},{20,28},{24,16},{28,20},{1,9},{5... | collective-permute-start | bytes 442376 | tf_op jit(solution)/shard_map/ppermute | solution.py:269
  49.5 18.7 %collective-permute-start.11 = (f32[288,128]{1,0:T(8,128)S(1)}, f32[288,128]{1,0:T(8,128)S(1)}, u32[]{:S(2)}, u32[]{:S(2)}) collective-permute-start(f32[288,128]{1,0:T(8,128)S(1)} %get-tuple-element.73), channel_id=1, source_target_pairs={{0,16},{4,20},{8,24},{12,28},{16,0},{20,4},{24,8},{28,12},{1,17},{... | collective-permute-start | bytes 442376 | tf_op jit(solution)/shard_map/ppermute | solution.py:269
  52.3 20.4 %collective-permute-start.12 = (f32[288,128]{1,0:T(8,128)S(1)}, f32[288,128]{1,0:T(8,128)S(1)}, u32[]{:S(2)}, u32[]{:S(2)}) collective-permute-start(f32[288,128]{1,0:T(8,128)S(1)} %get-tuple-element.74), channel_id=1, source_target_pairs={{0,24},{4,28},{8,16},{12,20},{16,8},{20,12},{24,0},{28,4},{1,25},{... | collective-permute-start | bytes 442376 | tf_op jit(solution)/shard_map/ppermute | solution.py:269
  56.3 26.8 %collective-permute-start.35 = (f32[6,48,128]{2,1,0:T(8,128)S(1)}, f32[6,48,128]{2,1,0:T(8,128)S(1)}, u32[]{:S(2)}, u32[]{:S(2)}) collective-permute-start(f32[6,48,128]{2,1,0:T(8,128)S(1)} %get-tuple-element.104), channel_id=1, source_target_pairs={{0,1},{1,0},{2,3},{3,2},{4,5},{5,4},{6,7},{7,6},{8,9},{9,8},{10,11... | collective-permute-start | bytes 442376 | tf_op jit(solution)/shard_map/ppermute | solution.py:269
  65.6 20.1 %collective-permute-start.36 = (f32[6,48,128]{2,1,0:T(8,128)S(1)}, f32[6,48,128]{2,1,0:T(8,128)S(1)}, u32[]{:S(2)}, u32[]{:S(2)}) collective-permute-start(f32[6,48,128]{2,1,0:T(8,128)S(1)} %get-tuple-element.105), channel_id=1, source_target_pairs={{0,2},{1,3},{2,0},{3,1},{4,6},{5,7},{6,4},{7,5},{8,10},{9,11},{10,... | collective-permute-start | bytes 442376 | tf_op jit(solution)/shard_map/ppermute | solution.py:269
  67.1 19.1 %collective-permute-start.4 = (f32[288,128]{1,0:T(8,128)S(1)}, f32[288,128]{1,0:T(8,128)S(1)}, u32[]{:S(2)}, u32[]{:S(2)}) collective-permute-start(f32[288,128]{1,0:T(8,128)S(1)} %get-tuple-element.63), channel_id=1, source_target_pairs={{0,8},{4,12},{8,0},{12,4},{16,24},{20,28},{24,16},{28,20},{1,9},{5... | collective-permute-start | bytes 442376 | tf_op jit(solution)/shard_map/ppermute | solution.py:269
  68.3 18.4 %collective-permute-start.5 = (f32[288,128]{1,0:T(8,128)S(1)}, f32[288,128]{1,0:T(8,128)S(1)}, u32[]{:S(2)}, u32[]{:S(2)}) collective-permute-start(f32[288,128]{1,0:T(8,128)S(1)} %get-tuple-element.64), channel_id=1, source_target_pairs={{0,16},{4,20},{8,24},{12,28},{16,0},{20,4},{24,8},{28,12},{1,17},{... | collective-permute-start | bytes 442376 | tf_op jit(solution)/shard_map/ppermute | solution.py:269
  72.7 16.5 %collective-permute-start.6 = (f32[288,128]{1,0:T(8,128)S(1)}, f32[288,128]{1,0:T(8,128)S(1)}, u32[]{:S(2)}, u32[]{:S(2)}) collective-permute-start(f32[288,128]{1,0:T(8,128)S(1)} %get-tuple-element.65), channel_id=1, source_target_pairs={{0,24},{4,28},{8,16},{12,20},{16,8},{20,12},{24,0},{28,4},{1,25},{... | collective-permute-start | bytes 442376 | tf_op jit(solution)/shard_map/ppermute | solution.py:269
  83.1 8.3 %collective-permute-start.37 = (f32[6,48,128]{2,1,0:T(8,128)S(1)}, f32[6,48,128]{2,1,0:T(8,128)S(1)}, u32[]{:S(2)}, u32[]{:S(2)}) collective-permute-start(f32[6,48,128]{2,1,0:T(8,128)S(1)} %get-tuple-element.106), channel_id=1, source_target_pairs={{0,3},{1,2},{2,1},{3,0},{4,7},{5,6},{6,5},{7,4},{8,11},{9,10},{10,... | collective-permute-start | bytes 442376 | tf_op jit(solution)/shard_map/ppermute | solution.py:269
  85.7 8.3 %collective-permute-start.22 = (f32[6,48,128]{2,1,0:T(8,128)S(1)}, f32[6,48,128]{2,1,0:T(8,128)S(1)}, u32[]{:S(2)}, u32[]{:S(2)}) collective-permute-start(f32[6,48,128]{2,1,0:T(8,128)S(1)} %get-tuple-element.88), channel_id=1, source_target_pairs={{0,1},{1,0},{2,3},{3,2},{4,5},{5,4},{6,7},{7,6},{8,9},{9,8},{10,11... | collective-permute-start | bytes 442376 | tf_op jit(solution)/shard_map/ppermute | solution.py:269
  86.1 8.4 %collective-permute-start.23 = (f32[6,48,128]{2,1,0:T(8,128)S(1)}, f32[6,48,128]{2,1,0:T(8,128)S(1)}, u32[]{:S(2)}, u32[]{:S(2)}) collective-permute-start(f32[6,48,128]{2,1,0:T(8,128)S(1)} %get-tuple-element.89), channel_id=1, source_target_pairs={{0,2},{1,3},{2,0},{3,1},{4,6},{5,7},{6,4},{7,5},{8,10},{9,11},{10,... | collective-permute-start | bytes 442376 | tf_op jit(solution)/shard_map/ppermute | solution.py:269
  86.7 10.8 %collective-permute-start.24 = (f32[6,48,128]{2,1,0:T(8,128)S(1)}, f32[6,48,128]{2,1,0:T(8,128)S(1)}, u32[]{:S(2)}, u32[]{:S(2)}) collective-permute-start(f32[6,48,128]{2,1,0:T(8,128)S(1)} %get-tuple-element.90), channel_id=1, source_target_pairs={{0,3},{1,2},{2,1},{3,0},{4,7},{5,6},{6,5},{7,4},{8,11},{9,10},{10,... | collective-permute-start | bytes 442376 | tf_op jit(solution)/shard_map/ppermute | solution.py:269
  89.2 11.1 %collective-permute-start.13 = (f32[6,48,128]{2,1,0:T(8,128)S(1)}, f32[6,48,128]{2,1,0:T(8,128)S(1)}, u32[]{:S(2)}, u32[]{:S(2)}) collective-permute-start(f32[6,48,128]{2,1,0:T(8,128)S(1)} %get-tuple-element.76), channel_id=1, source_target_pairs={{0,1},{1,0},{2,3},{3,2},{4,5},{5,4},{6,7},{7,6},{8,9},{9,8},{10,11... | collective-permute-start | bytes 442376 | tf_op jit(solution)/shard_map/ppermute | solution.py:269
  91.4 15.9 %collective-permute-start.7 = (f32[6,48,128]{2,1,0:T(8,128)S(1)}, f32[6,48,128]{2,1,0:T(8,128)S(1)}, u32[]{:S(2)}, u32[]{:S(2)}) collective-permute-start(f32[6,48,128]{2,1,0:T(8,128)S(1)} %get-tuple-element.68), channel_id=1, source_target_pairs={{0,1},{1,0},{2,3},{3,2},{4,5},{5,4},{6,7},{7,6},{8,9},{9,8},{10,11... | collective-permute-start | bytes 442376 | tf_op jit(solution)/shard_map/ppermute | solution.py:269
  94.0 9.4 %collective-permute-start.14 = (f32[6,48,128]{2,1,0:T(8,128)S(1)}, f32[6,48,128]{2,1,0:T(8,128)S(1)}, u32[]{:S(2)}, u32[]{:S(2)}) collective-permute-start(f32[6,48,128]{2,1,0:T(8,128)S(1)} %get-tuple-element.77), channel_id=1, source_target_pairs={{0,2},{1,3},{2,0},{3,1},{4,6},{5,7},{6,4},{7,5},{8,10},{9,11},{10,... | collective-permute-start | bytes 442376 | tf_op jit(solution)/shard_map/ppermute | solution.py:269
  94.5 11.6 %collective-permute-start.15 = (f32[6,48,128]{2,1,0:T(8,128)S(1)}, f32[6,48,128]{2,1,0:T(8,128)S(1)}, u32[]{:S(2)}, u32[]{:S(2)}) collective-permute-start(f32[6,48,128]{2,1,0:T(8,128)S(1)} %get-tuple-element.78), channel_id=1, source_target_pairs={{0,3},{1,2},{2,1},{3,0},{4,7},{5,6},{6,5},{7,4},{8,11},{9,10},{10,... | collective-permute-start | bytes 442376 | tf_op jit(solution)/shard_map/ppermute | solution.py:269
  97.5 10.7 %collective-permute-start.8 = (f32[6,48,128]{2,1,0:T(8,128)S(1)}, f32[6,48,128]{2,1,0:T(8,128)S(1)}, u32[]{:S(2)}, u32[]{:S(2)}) collective-permute-start(f32[6,48,128]{2,1,0:T(8,128)S(1)} %get-tuple-element.69), channel_id=1, source_target_pairs={{0,2},{1,3},{2,0},{3,1},{4,6},{5,7},{6,4},{7,5},{8,10},{9,11},{10,... | collective-permute-start | bytes 442376 | tf_op jit(solution)/shard_map/ppermute | solution.py:269
  100.3 7.8 %collective-permute-start.9 = (f32[6,48,128]{2,1,0:T(8,128)S(1)}, f32[6,48,128]{2,1,0:T(8,128)S(1)}, u32[]{:S(2)}, u32[]{:S(2)}) collective-permute-start(f32[6,48,128]{2,1,0:T(8,128)S(1)} %get-tuple-element.70), channel_id=1, source_target_pairs={{0,3},{1,2},{2,1},{3,0},{4,7},{5,6},{6,5},{7,4},{8,11},{9,10},{10,... | collective-permute-start | bytes 442376 | tf_op jit(solution)/shard_map/ppermute | solution.py:269
  (6 other events, 34.4 us)
